TPU v7x, 32 devices: a whole 2x2x4 slice. The times are simulated.
32 devices in a mesh: row: 8 (over z, y), col: 4 (over x, core).
Axes of the slice: x: 2, y: 2, z: 4, core: 2. Of those that a mesh axis runs over, the one named last changes fastest.
Arguments:
- matrix: float32 [4096, 4096], P('row', 'col'), may hold values from -0.92 to 1.92, as said below
Outputs:
- inverse: float32 [4096, 4096], P('row', 'col')
- residual_norms: float32 [4], replicated
Inputs may be any that keep to these rules, and one draw needn't show every extreme that they name: matrix is exactly symmetric and positive definite; all its eigenvalues lie between 0.08 and 1.92.
All inputs are finite; a program needn't handle non-finite values.
Results may differ from a plain program's by a relative error of at most 0.0017.
The roundings to bfloat16 on the way count: a program that leaves them out, or rounds other values in their place, can miss the bound.
Values may be sent and summed in bfloat16 or wider, within the bound.
A program may use at most 64 MiB of HBM per device.

v0:
```python
import jax
import jax.numpy as jnp
from jax import lax
from jax.sharding import PartitionSpec as P

ITERS = 4


def rounded(value):
    return lax.reduce_precision(value, 8, 7)


def first_iterate(panel, scale_low, row_start, col_start):
    rows = row_start + lax.broadcasted_iota(jnp.int32, panel.shape, 0)
    cols = col_start + lax.broadcasted_iota(jnp.int32, panel.shape, 1)
    eye = (rows == cols).astype(jnp.float32)
    shift = rounded(eye + (eye - scale_low * panel.astype(jnp.float32)))
    return (scale_low * shift).astype(jnp.bfloat16)


def transpose_blocks(block, row_size, col_size):
    ratio = row_size // col_size
    side = block.shape[0]
    row_index = lax.axis_index("row")
    pieces = []
    for turn in range(ratio):
        pairs = []
        for row in range(row_size):
            for col in range(col_size):
                target_row = ratio * col + (row + turn) % ratio
                pairs.append((row * col_size + col, target_row * col_size + row // ratio))
        half = lax.rem(row_index + turn, ratio)
        piece = lax.dynamic_slice_in_dim(block, half * side, side, axis=1)
        pieces.append(lax.ppermute(piece, ("row", "col"), pairs).T)
    out = jnp.zeros_like(block)
    for turn in range(ratio):
        half = lax.rem(row_index - turn + ratio, ratio)
        out = lax.dynamic_update_slice_in_dim(out, pieces[turn], half * side, axis=1)
    return out


def shards(matrix):
    row_count, col_count = matrix.shape
    row_size, col_size = (lax.axis_size("row"), lax.axis_size("col"))
    order = col_count * col_size
    row_start = lax.axis_index("row") * row_count
    col_start = lax.axis_index("col") * col_count
    global_rows = row_start + lax.broadcasted_iota(jnp.int32, (row_count, col_count), 0)
    global_cols = col_start + lax.broadcasted_iota(jnp.int32, (row_count, col_count), 1)
    eye_block = (global_rows == global_cols).astype(jnp.float32)
    mat_low = matrix.astype(jnp.bfloat16)
    sq_total = lax.psum(jnp.sum(matrix * matrix), ("row", "col"))
    panel_rows = lax.all_gather(mat_low, "col", axis=1, tiled=True)
    panel_cols = lax.all_gather(mat_low, "row", axis=0, tiled=True)
    start_scale = jnp.sqrt(jnp.float32(order)) / jnp.sqrt(sq_total)
    scale_low = rounded(start_scale)
    residual = eye_block - scale_low * rounded(matrix)
    partial_list = [jnp.sum(residual * residual)]
    iterate_rows = first_iterate(panel_rows, scale_low, row_start, 0)
    iterate_cols = first_iterate(panel_cols, scale_low, 0, col_start)
    for iteration in range(1, ITERS):
        product = jnp.dot(iterate_rows, panel_cols, preferred_element_type=jnp.float32)
        residual = eye_block - product
        partial_list.append(jnp.sum(residual * residual))
        shift_low = (eye_block + residual).astype(jnp.bfloat16)
        current = jnp.dot(
            lax.all_gather(shift_low, "col", axis=1, tiled=True),
            iterate_cols,
            preferred_element_type=jnp.float32,
        )
        if iteration < ITERS - 1:
            cur_low = current.astype(jnp.bfloat16)
            iterate_rows = lax.all_gather(cur_low, "col", axis=1, tiled=True)
            iterate_cols = lax.all_gather(cur_low, "row", axis=0, tiled=True)
    summed = lax.psum(jnp.stack(partial_list), ("row", "col"))
    residual_norms = jnp.sqrt(summed / order)
    return (transpose_blocks(current, row_size, col_size), residual_norms)


def solution(mesh):
    in_specs = (P("row", "col"),)
    out_specs = (P("row", "col"), P())
    return jax.shard_map(shards, mesh=mesh, in_specs=in_specs, out_specs=out_specs, check_vma=False)
```

profile of v0, /device:TPU:0, one launch (start us, length us, event | category | flops | bytes accessed | tf_op | source)
XLA Modules:
  0.0 790.7 jit_solution(10998236796299218012)
XLA Ops:
  7.2 4.3 multiply_reduce_fusion.3
  11.5 0.7 all-gather.12.cloned.1.call-update
  12.3 42.5 %psum.14 = f32[]{:T(128)} all-reduce(f32[]{:T(128)} %get-tuple-element.9), channel_id=1, replica_groups=mesh['row'=8,'col'=4] {'row','col'}, use_global_device_ids=true, to_apply=%region_1.0 | all-reduce | flops 1 | bytes 8 | tf_op jit(solution)/shard_map/psum | solution.py:52
  56.0 120.3 %all-gather.12.cloned.1.call-done = bf16[4096,1024]{1,0:T(8,128)(2,1)} async-done(((bf16[512,1024]{1,0:T(8,128)(2,1)}), bf16[4096,1024]{1,0:T(8,128)(2,1)}) %all-gather.12.cloned.1.call-update) | async-done | bytes 8388624 | tf_op jit(solution)/shard_map/all_gather | solution.py:54
  176.3 12.1 %fusion.12 = (bf16[512,1024]{1,0:T(8,128)(2,1)}, f32[512,1024]{1,0:T(8,128)}) fusion(s32[1024]{0:T(1024)S(1)} %iota_add_fusion, s32[512]{0:T(512)S(1)} %iota_add_fusion.1, bf16[4096,1024]{1,0:T(8,128)(2,1)} %all-gather.12.cloned.1.call-done, bf16[512,4096]{1,0:T(8,128)(2,1)} %all-gather.10.cloned.1.call-done, f32[]{:T(128)} %reduce_precision.12), kind=kOutput, calls=%fused_computation.21 | convolution fusion | flops 4316463104 | bytes 15734788 | tf_op jit(solution)/shard_map/dot_general | solution.py:62
  188.5 32.7 %all-gather.14.cloned.1.call-done = bf16[512,4096]{1,0:T(8,128)(2,1)} async-done(((bf16[512,1024]{1,0:T(8,128)(2,1)}), bf16[512,4096]{1,0:T(8,128)(2,1)}) %all-gather.14.cloned.1.call-update) | async-done | bytes 4194320 | tf_op jit(solution)/shard_map/all_gather | solution.py:67
  221.3 12.0 %fusion.17 = bf16[512,1024]{1,0:T(8,128)(2,1)} fusion(bf16[512,4096]{1,0:T(8,128)(2,1)} %all-gather.14.cloned.1.call-done, bf16[4096,1024]{1,0:T(8,128)(2,1)} %all-gather.12.cloned.1.call-done, s32[1024]{0:T(1024)S(1)} %iota_add_fusion, f32[]{:T(128)} %reduce_precision.12), kind=kOutput, calls=%fused_computation.30 | convolution fusion | flops 4333240320 | bytes 13635588 | tf_op jit(solution)/shard_map/dot_general | solution.py:66
  233.5 34.4 %all-gather.16.cloned.1.call-done = bf16[512,4096]{1,0:T(8,128)(2,1)} async-done(((bf16[512,1024]{1,0:T(8,128)(2,1)}), bf16[512,4096]{1,0:T(8,128)(2,1)}) %all-gather.16.cloned.1.call-update) | async-done | bytes 4194320 | tf_op jit(solution)/shard_map/all_gather | solution.py:73
  267.9 10.9 %fusion.13 = (bf16[512,1024]{1,0:T(8,128)(2,1)}, f32[512,1024]{1,0:T(8,128)}) fusion(s32[1024]{0:T(1024)S(1)} %iota_add_fusion, s32[512]{0:T(512)S(1)} %iota_add_fusion.1, bf16[512,4096]{1,0:T(8,128)(2,1)} %all-gather.16.cloned.1.call-done, bf16[4096,1024]{1,0:T(8,128)(2,1)} %all-gather.12.cloned.1.call-done), kind=kOutput, calls=%fused_computation.22 | convolution fusion | flops 4297588736 | bytes 15734784 | tf_op jit(solution)/shard_map/dot_general | solution.py:62
  278.8 0.5 all-gather.20.cloned.1.call-update
  279.4 34.0 %all-gather.18.cloned.1.call-done = bf16[512,4096]{1,0:T(8,128)(2,1)} async-done(((bf16[512,1024]{1,0:T(8,128)(2,1)}), bf16[512,4096]{1,0:T(8,128)(2,1)}) %all-gather.18.cloned.1.call-update) | async-done | bytes 4194320 | tf_op jit(solution)/shard_map/all_gather | solution.py:67
  313.4 126.5 %all-gather.20.cloned.1.call-done = bf16[4096,1024]{1,0:T(8,128)(2,1)} async-done(((bf16[512,1024]{1,0:T(8,128)(2,1)}), bf16[4096,1024]{1,0:T(8,128)(2,1)}) %all-gather.20.cloned.1.call-update) | async-done | bytes 8388624 | tf_op jit(solution)/shard_map/all_gather | solution.py:74
  439.9 10.2 %convolution_convert_fusion = bf16[512,1024]{1,0:T(8,128)(2,1)} fusion(bf16[512,4096]{1,0:T(8,128)(2,1)} %all-gather.18.cloned.1.call-done, bf16[4096,1024]{1,0:T(8,128)(2,1)} %all-gather.20.cloned.1.call-done), kind=kOutput, calls=%fused_computation.31 | convolution fusion | flops 4295491584 | bytes 13631488 | tf_op jit(solution)/shard_map/dot_general | solution.py:66
  450.1 32.7 %all-gather.22.cloned.1.call-done = bf16[512,4096]{1,0:T(8,128)(2,1)} async-done(((bf16[512,1024]{1,0:T(8,128)(2,1)}), bf16[512,4096]{1,0:T(8,128)(2,1)}) %all-gather.22.cloned.1.call-update) | async-done | bytes 4194320 | tf_op jit(solution)/shard_map/all_gather | solution.py:73
  482.8 13.2 %fusion.16 = (f32[]{:T(128)}, f32[]{:T(128)}, f32[]{:T(128)}, f32[]{:T(128)}, bf16[512,1024]{1,0:T(8,128)(2,1)}) fusion(f32[512,1024]{1,0:T(8,128)S(1)} %copy-done.1, f32[]{:T(128)} %reduce_precision.12, s32[1024]{0:T(1024)S(1)} %iota_add_fusion, s32[512]{0:T(512)S(1)} %iota_add_fusion.1, f32[512,1024]{1,0:T(8,128)} %get-tuple-element.14, ...), kind=kOutput, calls=%fused_computation.25 | convolution fusion | flops 4304404480 | bytes 19929108 | tf_op jit(solution)/shard_map/dot_general | solution.py:62
  496.8 33.9 %all-gather.24.cloned.1.call-done = bf16[512,4096]{1,0:T(8,128)(2,1)} async-done(((bf16[512,1024]{1,0:T(8,128)(2,1)}), bf16[512,4096]{1,0:T(8,128)(2,1)}) %all-gather.24.cloned.1.call-update) | async-done | bytes 4194320 | tf_op jit(solution)/shard_map/all_gather | solution.py:67
  530.6 126.6 %all-gather.26.cloned.1.call-done = bf16[4096,1024]{1,0:T(8,128)(2,1)} async-done(((bf16[512,1024]{1,0:T(8,128)(2,1)}), bf16[4096,1024]{1,0:T(8,128)(2,1)}) %all-gather.26.cloned.1.call-update) | async-done | bytes 8388624 | tf_op jit(solution)/shard_map/all_gather | solution.py:74
  657.3 8.1 %fusion.20 = f32[512,1024]{1,0:T(8,128)S(1)} fusion(bf16[512,4096]{1,0:T(8,128)(2,1)} %all-gather.24.cloned.1.call-done, bf16[4096,1024]{1,0:T(8,128)(2,1)} %all-gather.26.cloned.1.call-done), kind=kOutput, calls=%fused_computation.40 | convolution fusion | flops 4294967296 | bytes 14680064 | tf_op jit(solution)/shard_map/dot_general | solution.py:66
  665.7 1.6 collective-permute-start
  667.3 0.6 collective-permute-start.1
  667.8 2.5 pad_maximum_fusion
  670.4 109.5 %psum.15 = f32[4]{0:T(128)S(1)} all-reduce(f32[4]{0:T(128)S(1)} %pad_maximum_fusion), channel_id=1, replica_groups=mesh['row'=8,'col'=4] {'row','col'}, use_global_device_ids=true, to_apply=%region_6.0 | all-reduce | flops 4 | bytes 32 | tf_op jit(solution)/shard_map/psum | solution.py:75
  780.4 1.6 copy.3
  782.8 1.3 copy-done
  (30 shorter events, 2.9 us)
Async XLA Ops:
  7.2 48.9 %all-gather.10.cloned.1.call-start = ((), (), s32[]{:S(2)}) async-start(), calls=%async_computation | async-start | bytes 5242880 | tf_op jit(solution)/shard_map/all_gather | solution.py:53
  11.5 164.8 %all-gather.12.cloned.1.call-start = ((), (), s32[]{:S(2)}) async-start(), calls=%async_computation.1 | async-start | bytes 9437184 | tf_op jit(solution)/shard_map/all_gather | solution.py:54
  12.3 209.0 %all-gather.14.cloned.1.call-start = ((), (), s32[]{:S(2)}) async-start(), calls=%async_computation.2 | async-start | bytes 5242880 | tf_op jit(solution)/shard_map/all_gather | solution.py:67
  188.5 79.4 %all-gather.16.cloned.1.call-start = ((), (), s32[]{:S(2)}) async-start(), calls=%async_computation.3 | async-start | bytes 5242880 | tf_op jit(solution)/shard_map/all_gather | solution.py:73
  233.3 80.1 %all-gather.18.cloned.1.call-start = ((), (), s32[]{:S(2)}) async-start(), calls=%async_computation.4 | async-start | bytes 5242880 | tf_op jit(solution)/shard_map/all_gather | solution.py:67
  278.8 161.1 %all-gather.20.cloned.1.call-start = ((), (), s32[]{:S(2)}) async-start(), calls=%async_computation.5 | async-start | bytes 9437184 | tf_op jit(solution)/shard_map/all_gather | solution.py:74
  279.3 203.5 %copy-start.1 = (f32[512,1024]{1,0:T(8,128)S(1)}, f32[512,1024]{1,0:T(8,128)}, u32[]{:S(2)}) copy-start(f32[512,1024]{1,0:T(8,128)} %param.1) | copy-start | bytes 6291460
  279.4 203.5 %all-gather.22.cloned.1.call-start = ((), (), s32[]{:S(2)}) async-start(), calls=%async_computation.6 | async-start | bytes 5242880 | tf_op jit(solution)/shard_map/all_gather | solution.py:73
  450.1 80.6 %all-gather.24.cloned.1.call-start = ((), (), s32[]{:S(2)}) async-start(), calls=%async_computation.7 | async-start | bytes 5242880 | tf_op jit(solution)/shard_map/all_gather | solution.py:67
  496.0 161.3 %all-gather.26.cloned.1.call-start = ((), (), s32[]{:S(2)}) async-start(), calls=%async_computation.8 | async-start | bytes 9437184 | tf_op jit(solution)/shard_map/all_gather | solution.py:74
  665.7 114.8 %collective-permute-start = (f32[512,512]{1,0:T(8,128)S(1)}, f32[512,512]{1,0:T(8,128)}, u32[]{:S(2)}, u32[]{:S(2)}) collective-permute-start(f32[512,512]{1,0:T(8,128)S(1)} %get-tuple-element.8), channel_id=1, source_target_pairs={{0,0},{1,8},{2,16},{3,24},{4,4},{5,12},{6,20},{7,28},{8,1},{9,9},{... | collective-permute-start | bytes 3145736 | tf_op jit(solution)/shard_map/ppermute | solution.py:34
  667.3 114.7 %collective-permute-start.1 = (f32[512,512]{1,0:T(8,128)S(1)}, f32[512,512]{1,0:T(8,128)S(1)}, u32[]{:S(2)}, u32[]{:S(2)}) collective-permute-start(f32[512,512]{1,0:T(8,128)S(1)} %get-tuple-element.7), channel_id=1, source_target_pairs={{0,4},{1,12},{2,20},{3,28},{4,0},{5,8},{6,16},{7,24},{8,5},{9,13},... | collective-permute-start | bytes 3145736 | tf_op jit(solution)/shard_map/ppermute | solution.py:34
  782.8 1.3 copy-start
Sparse Core Ops, SparseCore 0:
  11.6 37.4 all-gather.9
  51.8 124.4 all-gather.11
  188.6 32.6 all-gather.13
  233.4 34.4 all-gather.15
  278.9 34.4 all-gather.17
  315.4 124.4 all-gather.19
  450.2 32.6 all-gather.21
  496.1 34.4 all-gather.23
  532.8 124.4 all-gather.25
where the time goes:
time: 791 us
  waiting for transfers between devices  543 us (69%)
  blocking collectives  152 us (19%)
  matrix products  66.4 us (8%)
  between operations  15.1 us (2%)
    all_gather x2, waiting for transfers between devices, shards(): iterate_cols = lax.all_gather(cur_low, 'row', axis=0, tiled=True)  253 us
    all_gather x1, waiting for transfers between devices, shards(): panel_cols = lax.all_gather(mat_low, 'row', axis=0, tiled=True)  120 us
    psum x1, blocking collectives, shards(): summed = lax.psum(jnp.stack(partial_list), ('row', 'col'))  110 us
    all_gather x3, waiting for transfers between devices, shards(): lax.all_gather(shift_low, 'col', axis=1, tiled=True)  101 us
    all_gather x2, waiting for transfers between devices, shards(): iterate_rows = lax.all_gather(cur_low, 'col', axis=1, tiled=True)  67.1 us
    psum x1, blocking collectives, shards(): sq_total = lax.psum(jnp.sum(matrix * matrix), ('row', 'col'))  42.5 us
    dot_general x3, matrix products, shards(): jnp.dot(iterate_rows, panel_cols, preferred_element_type=jnp.float32)  36.2 us
    dot_general x3, matrix products, shards(): jnp.dot(lax.all_gather(shift_low, 'col', axis=1, tiled=True), iterate_col...  30.3 us
  transfers between devices with their start and end apart: 11, of which 8 were waited for; matrix products, arithmetic and copies ran while one was open for 1% of the time, Pallas kernels for 0%

commit v1 on v0

--- a/solution.py
+++ b/solution.py
@@ -4,6 +4,17 @@
 from jax.sharding import PartitionSpec as P
 
 ITERS = 4
+
+
+def gather_by_hops(x, axis, dim):
+    size = lax.axis_size(axis)
+    route = [(i, (i + 1) % size) for i in range(size)]
+    parts = [x]
+    for reach in range(1, size):
+        parts = [lax.ppermute(parts[0], axis, route), *parts]
+    full = jnp.concatenate(parts, axis=dim)
+    shift = (lax.axis_index(axis) + 1) * parts[-1].shape[dim]
+    return jnp.roll(full, shift, axis=dim)
 
 
 def rounded(value):
@@ -71,7 +82,7 @@
         if iteration < ITERS - 1:
             cur_low = current.astype(jnp.bfloat16)
             iterate_rows = lax.all_gather(cur_low, "col", axis=1, tiled=True)
-            iterate_cols = lax.all_gather(cur_low, "row", axis=0, tiled=True)
+            iterate_cols = gather_by_hops(cur_low, "row", 0)
     summed = lax.psum(jnp.stack(partial_list), ("row", "col"))
     residual_norms = jnp.sqrt(summed / order)
     return (transpose_blocks(current, row_size, col_size), residual_norms)

time: 791 us -> 734 us (0.928)
  waiting for transfers between devices: 543 us -> 464 us
  local copies, waits for them, and re-layouts: 3.86 us -> 36.1 us
  blocking collectives: 152 us -> 139 us
    ppermute x0 -> x14, waiting for transfers between devices: none -> 310 us  [gather_by_hops(): parts = [lax.ppermute(parts[0], axis, route), *parts]]
    all_gather x2 -> x0, waiting for transfers between devices: 253 us -> none  [shards(): iterate_cols = lax.all_gather(cur_low, 'row', axis=0, tiled=True)]
    all_gather x3, waiting for transfers between devices: 101 us -> 32.7 us  [shards(): lax.all_gather(shift_low, 'col', axis=1, tiled=True)]
    all_gather x2, waiting for transfers between devices: 67.1 us -> 0.01 us  [shards(): iterate_rows = lax.all_gather(cur_low, 'col', axis=1, tiled=True)]
    unnamed x4 -> x28, local copies, waits for them, and re-layouts: 1.32 us -> 31.4 us
    psum x1, blocking collectives: 110 us -> 96.9 us  [shards(): summed = lax.psum(jnp.stack(partial_list), ('row', 'col'))]
  transfers between devices with their start and end apart: 11 -> 23, of which waited for: 8 -> 16; matrix products, arithmetic and copies ran while one was open for 1% -> 8% of each run, Pallas kernels for 0% -> 0%
where the time goes in v1:
time: 734 us; the launch traced here: 733 us
  waiting for transfers between devices  464 us (63%)
  blocking collectives  139 us (19%)
  matrix products  67 us (9%)
  local copies, waits for them, and re-layouts  36.1 us (5%)
  between operations  15.4 us (2%)
    ppermute x14, waiting for transfers between devices, gather_by_hops(): parts = [lax.ppermute(parts[0], axis, route), *parts]  310 us
    all_gather x1, waiting for transfers between devices, shards(): panel_cols = lax.all_gather(mat_low, 'row', axis=0, tiled=True)  120 us
    psum x1, blocking collectives, shards(): summed = lax.psum(jnp.stack(partial_list), ('row', 'col'))  96.9 us
    psum x1, blocking collectives, shards(): sq_total = lax.psum(jnp.sum(matrix * matrix), ('row', 'col'))  42.5 us
    dot_general x3, matrix products, shards(): jnp.dot(iterate_rows, panel_cols, preferred_element_type=jnp.float32)  36.2 us
    all_gather x3, waiting for transfers between devices, shards(): lax.all_gather(shift_low, 'col', axis=1, tiled=True)  32.7 us
    unnamed x28, local copies, waits for them, and re-layouts  31.4 us
    dot_general x3, matrix products, shards(): jnp.dot(lax.all_gather(shift_low, 'col', axis=1, tiled=True), iterate_col...  30.8 us
  transfers between devices with their start and end apart: 23, of which 16 were waited for; matrix products, arithmetic and copies ran while one was open for 8% of the time, Pallas kernels for 0%

profile of v1, /device:TPU:0, one launch (start us, length us, event | category | flops | bytes accessed | tf_op | source)
XLA Modules:
  0.0 732.9 jit_solution(14986204761664931840)
XLA Ops:
  12.3 42.5 %psum.14 = f32[]{:T(128)} all-reduce(f32[]{:T(128)} %get-tuple-element.10), channel_id=1, replica_groups=mesh['row'=8,'col'=4] {'row','col'}, use_global_device_ids=true, to_apply=%region_1.0 | all-reduce | flops 1 | bytes 8 | tf_op jit(solution)/shard_map/psum | solution.py:63
  56.0 120.3 %all-gather.10.cloned.1.call-done = bf16[4096,1024]{1,0:T(8,128)(2,1)} async-done(((bf16[512,1024]{1,0:T(8,128)(2,1)}), bf16[4096,1024]{1,0:T(8,128)(2,1)}) %all-gather.10.cloned.1.call-update) | async-done | bytes 8388624 | tf_op jit(solution)/shard_map/all_gather | solution.py:65
  176.3 12.1 %fusion.18 = (bf16[512,1024]{1,0:T(8,128)(2,1)}, f32[512,1024]{1,0:T(8,128)}) fusion(s32[1024]{0:T(1024)S(1)} %iota_add_fusion, s32[512]{0:T(512)S(1)} %iota_add_fusion.1, bf16[4096,1024]{1,0:T(8,128)(2,1)} %all-gather.10.cloned.1.call-done, bf16[512,4096]{1,0:T(8,128)(2,1)} %all-gather.8.cloned.1.call-done, f32[]{:T(128)} %reduce_precision.12), kind=kOutput, calls=%fused_computation.29 | convolution fusion | flops 4316463104 | bytes 15734788 | tf_op jit(solution)/shard_map/dot_general | solution.py:73
  188.5 32.7 %all-gather.12.cloned.1.call-done = bf16[512,4096]{1,0:T(8,128)(2,1)} async-done(((bf16[512,1024]{1,0:T(8,128)(2,1)}), bf16[512,4096]{1,0:T(8,128)(2,1)}) %all-gather.12.cloned.1.call-update) | async-done | bytes 4194320 | tf_op jit(solution)/shard_map/all_gather | solution.py:78
  221.2 11.9 %fusion.23 = bf16[512,1024]{1,0:T(8,128)(2,1)} fusion(bf16[512,4096]{1,0:T(8,128)(2,1)} %all-gather.12.cloned.1.call-done, bf16[4096,1024]{1,0:T(8,128)(2,1)} %all-gather.10.cloned.1.call-done, s32[1024]{0:T(1024)S(1)} %iota_add_fusion, f32[]{:T(128)} %reduce_precision.12), kind=kOutput, calls=%fused_computation.38 | convolution fusion | flops 4333240320 | bytes 13635588 | tf_op jit(solution)/shard_map/dot_general | solution.py:77
  234.9 26.7 %collective-permute-done = bf16[512,1024]{1,0:T(8,128)(2,1)S(1)} collective-permute-done((bf16[512,1024]{1,0:T(8,128)(2,1)}, bf16[512,1024]{1,0:T(8,128)(2,1)S(1)}, u32[]{:S(2)}, u32[]{:S(2)}) %collective-permute-start) | collective-permute-done | bytes 1048608 | tf_op jit(solution)/shard_map/ppermute | solution.py:14
  261.7 27.1 %collective-permute-done.1 = bf16[512,1024]{1,0:T(8,128)(2,1)S(1)} collective-permute-done((bf16[512,1024]{1,0:T(8,128)(2,1)S(1)}, bf16[512,1024]{1,0:T(8,128)(2,1)S(1)}, u32[]{:S(2)}, u32[]{:S(2)}) %collective-permute-start.1) | collective-permute-done | bytes 1048608 | tf_op jit(solution)/shard_map/ppermute | solution.py:14
  288.8 10.9 %fusion.19 = (bf16[512,1024]{1,0:T(8,128)(2,1)}, f32[512,1024]{1,0:T(8,128)}) fusion(s32[1024]{0:T(1024)S(1)} %iota_add_fusion, s32[512]{0:T(512)S(1)} %iota_add_fusion.1, bf16[512,4096]{1,0:T(8,128)(2,1)} %all-gather.14.cloned.1.call-done, bf16[4096,1024]{1,0:T(8,128)(2,1)} %all-gather.10.cloned.1.call-done), kind=kOutput, calls=%fused_computation.30 | convolution fusion | flops 4297588736 | bytes 15734784 | tf_op jit(solution)/shard_map/dot_general | solution.py:73
  299.9 15.4 %collective-permute-done.2 = bf16[512,1024]{1,0:T(8,128)(2,1)} collective-permute-done((bf16[512,1024]{1,0:T(8,128)(2,1)S(1)}, bf16[512,1024]{1,0:T(8,128)(2,1)}, u32[]{:S(2)}, u32[]{:S(2)}) %collective-permute-start.2) | collective-permute-done | bytes 1048608 | tf_op jit(solution)/shard_map/ppermute | solution.py:14
  315.2 25.6 %collective-permute-done.3 = bf16[512,1024]{1,0:T(8,128)(2,1)S(1)} collective-permute-done((bf16[512,1024]{1,0:T(8,128)(2,1)}, bf16[512,1024]{1,0:T(8,128)(2,1)S(1)}, u32[]{:S(2)}, u32[]{:S(2)}) %collective-permute-start.3) | collective-permute-done | bytes 1048608 | tf_op jit(solution)/shard_map/ppermute | solution.py:14
  341.9 24.6 %collective-permute-done.4 = bf16[512,1024]{1,0:T(8,128)(2,1)S(1)} collective-permute-done((bf16[512,1024]{1,0:T(8,128)(2,1)S(1)}, bf16[512,1024]{1,0:T(8,128)(2,1)S(1)}, u32[]{:S(2)}, u32[]{:S(2)}) %collective-permute-start.4) | collective-permute-done | bytes 1048608 | tf_op jit(solution)/shard_map/ppermute | solution.py:14
  367.4 23.8 %collective-permute-done.5 = bf16[512,1024]{1,0:T(8,128)(2,1)} collective-permute-done((bf16[512,1024]{1,0:T(8,128)(2,1)S(1)}, bf16[512,1024]{1,0:T(8,128)(2,1)}, u32[]{:S(2)}, u32[]{:S(2)}) %collective-permute-start.5) | collective-permute-done | bytes 1048608 | tf_op jit(solution)/shard_map/ppermute | solution.py:14
  391.3 23.2 %collective-permute-done.6 = bf16[512,1024]{1,0:T(8,128)(2,1)} collective-permute-done((bf16[512,1024]{1,0:T(8,128)(2,1)}, bf16[512,1024]{1,0:T(8,128)(2,1)}, u32[]{:S(2)}, u32[]{:S(2)}) %collective-permute-start.6) | collective-permute-done | bytes 1048608 | tf_op jit(solution)/shard_map/ppermute | solution.py:14
  429.2 10.6 %fusion.26 = bf16[512,1024]{1,0:T(8,128)(2,1)} fusion(bf16[512,4096]{1,0:T(8,128)(2,1)} %all-gather.16.cloned.1.call-done, s32[]{:T(128)S(6)} %select_n.26, bf16[4096,1024]{1,0:T(8,128)(2,1)} %constant_dynamic-update-slice_fusion), kind=kOutput, calls=%fused_computation.39 | convolution fusion | flops 4312268800 | bytes 13631492 | tf_op jit(solution)/shard_map/dot_general | solution.py:77
  439.8 23.5 %collective-permute-done.7 = bf16[512,1024]{1,0:T(8,128)(2,1)S(1)} collective-permute-done((bf16[512,1024]{1,0:T(8,128)(2,1)}, bf16[512,1024]{1,0:T(8,128)(2,1)S(1)}, u32[]{:S(2)}, u32[]{:S(2)}) %collective-permute-start.7) | collective-permute-done | bytes 1048608 | tf_op jit(solution)/shard_map/ppermute | solution.py:14
  463.4 23.1 %collective-permute-done.8 = bf16[512,1024]{1,0:T(8,128)(2,1)} collective-permute-done((bf16[512,1024]{1,0:T(8,128)(2,1)S(1)}, bf16[512,1024]{1,0:T(8,128)(2,1)}, u32[]{:S(2)}, u32[]{:S(2)}) %collective-permute-start.8) | collective-permute-done | bytes 1048608 | tf_op jit(solution)/shard_map/ppermute | solution.py:14
  486.5 13.1 %fusion.22 = (f32[]{:T(128)}, f32[]{:T(128)}, f32[]{:T(128)}, f32[]{:T(128)}, bf16[512,1024]{1,0:T(8,128)(2,1)}) fusion(f32[512,1024]{1,0:T(8,128)S(1)} %copy-done.3, f32[]{:T(128)} %reduce_precision.12, s32[1024]{0:T(1024)S(1)} %iota_add_fusion, s32[512]{0:T(512)S(1)} %iota_add_fusion.1, f32[512,1024]{1,0:T(8,128)} %get-tuple-element.15, ...), kind=kOutput, calls=%fused_computation.33 | convolution fusion | flops 4304404480 | bytes 19929108 | tf_op jit(solution)/shard_map/dot_general | solution.py:73
  499.6 10.2 %collective-permute-done.9 = bf16[512,1024]{1,0:T(8,128)(2,1)} collective-permute-done((bf16[512,1024]{1,0:T(8,128)(2,1)}, bf16[512,1024]{1,0:T(8,128)(2,1)}, u32[]{:S(2)}, u32[]{:S(2)}) %collective-permute-start.9) | collective-permute-done | bytes 1048608 | tf_op jit(solution)/shard_map/ppermute | solution.py:14
  509.8 23.5 %collective-permute-done.10 = bf16[512,1024]{1,0:T(8,128)(2,1)S(1)} collective-permute-done((bf16[512,1024]{1,0:T(8,128)(2,1)}, bf16[512,1024]{1,0:T(8,128)(2,1)S(1)}, u32[]{:S(2)}, u32[]{:S(2)}) %collective-permute-start.10) | collective-permute-done | bytes 1048608 | tf_op jit(solution)/shard_map/ppermute | solution.py:14
  533.3 22.4 %collective-permute-done.11 = bf16[512,1024]{1,0:T(8,128)(2,1)S(1)} collective-permute-done((bf16[512,1024]{1,0:T(8,128)(2,1)S(1)}, bf16[512,1024]{1,0:T(8,128)(2,1)S(1)}, u32[]{:S(2)}, u32[]{:S(2)}) %collective-permute-start.11) | collective-permute-done | bytes 1048608 | tf_op jit(solution)/shard_map/ppermute | solution.py:14
  556.7 23.1 %collective-permute-done.12 = bf16[512,1024]{1,0:T(8,128)(2,1)} collective-permute-done((bf16[512,1024]{1,0:T(8,128)(2,1)S(1)}, bf16[512,1024]{1,0:T(8,128)(2,1)}, u32[]{:S(2)}, u32[]{:S(2)}) %collective-permute-start.12) | collective-permute-done | bytes 1048608 | tf_op jit(solution)/shard_map/ppermute | solution.py:14
  579.8 17.8 %collective-permute-done.13 = bf16[512,1024]{1,0:T(8,128)(2,1)} collective-permute-done((bf16[512,1024]{1,0:T(8,128)(2,1)}, bf16[512,1024]{1,0:T(8,128)(2,1)}, u32[]{:S(2)}, u32[]{:S(2)}) %collective-permute-start.13) | collective-permute-done | bytes 1048608 | tf_op jit(solution)/shard_map/ppermute | solution.py:14
  612.2 8.4 %fusion.7 = f32[512,1024]{1,0:T(8,128)S(1)} fusion(bf16[512,4096]{1,0:T(8,128)(2,1)} %all-gather.20.cloned.1.call-done, s32[]{:T(128)S(6)} %select_n.26, bf16[4096,1024]{1,0:T(8,128)(2,1)} %constant_dynamic-update-slice_fusion.8), kind=kOutput, calls=%fused_computation.14 | convolution fusion | flops 4311744512 | bytes 14680068 | tf_op jit(solution)/shard_map/dot_general | solution.py:77
  624.9 96.9 %psum.15 = f32[4]{0:T(128)S(1)} all-reduce(f32[4]{0:T(128)S(1)} %pad_maximum_fusion), channel_id=1, replica_groups=mesh['row'=8,'col'=4] {'row','col'}, use_global_device_ids=true, to_apply=%region_6.8 | all-reduce | flops 4 | bytes 32 | tf_op jit(solution)/shard_map/psum | solution.py:86
  (78 shorter events, 47.9 us)
Async XLA Ops:
  7.2 48.9 %all-gather.8.cloned.1.call-start = ((), (), s32[]{:S(2)}) async-start(), calls=%async_computation | async-start | bytes 5242880 | tf_op jit(solution)/shard_map/all_gather | solution.py:64
  11.5 164.8 %all-gather.10.cloned.1.call-start = ((), (), s32[]{:S(2)}) async-start(), calls=%async_computation.1 | async-start | bytes 9437184 | tf_op jit(solution)/shard_map/all_gather | solution.py:65
  12.3 209.0 %all-gather.12.cloned.1.call-start = ((), (), s32[]{:S(2)}) async-start(), calls=%async_computation.2 | async-start | bytes 5242880 | tf_op jit(solution)/shard_map/all_gather | solution.py:78
  188.4 100.4 %all-gather.14.cloned.1.call-start = ((), (), s32[]{:S(2)}) async-start(), calls=%async_computation.3 | async-start | bytes 5242880 | tf_op jit(solution)/shard_map/all_gather | solution.py:84
  233.2 196.0 %all-gather.16.cloned.1.call-start = ((), (), s32[]{:S(2)}) async-start(), calls=%async_computation.4 | async-start | bytes 5242880 | tf_op jit(solution)/shard_map/all_gather | solution.py:78
  233.4 28.3 %collective-permute-start = (bf16[512,1024]{1,0:T(8,128)(2,1)}, bf16[512,1024]{1,0:T(8,128)(2,1)S(1)}, u32[]{:S(2)}, u32[]{:S(2)}) collective-permute-start(bf16[512,1024]{1,0:T(8,128)(2,1)} %fusion.23), channel_id=1, source_target_pairs={{0,4},{4,8},{8,12},{12,16},{16,20},{20,24},{24,28},{28,0},{1,5},{5... | collective-permute-start | bytes 3145736 | tf_op jit(solution)/shard_map/ppermute | solution.py:14
  261.7 27.1 %collective-permute-start.1 = (bf16[512,1024]{1,0:T(8,128)(2,1)S(1)}, bf16[512,1024]{1,0:T(8,128)(2,1)S(1)}, u32[]{:S(2)}, u32[]{:S(2)}) collective-permute-start(bf16[512,1024]{1,0:T(8,128)(2,1)S(1)} %collective-permute-done), channel_id=1, source_target_pairs={{0,4},{4,8},{8,12},{12,16},{16,20},{20,24},{24,28},{28,0},{1,5},{5... | collective-permute-start | bytes 3145736 | tf_op jit(solution)/shard_map/ppermute | solution.py:14
  288.8 26.4 %collective-permute-start.2 = (bf16[512,1024]{1,0:T(8,128)(2,1)S(1)}, bf16[512,1024]{1,0:T(8,128)(2,1)}, u32[]{:S(2)}, u32[]{:S(2)}) collective-permute-start(bf16[512,1024]{1,0:T(8,128)(2,1)S(1)} %collective-permute-done.1), channel_id=1, source_target_pairs={{0,4},{4,8},{8,12},{12,16},{16,20},{20,24},{24,28},{28,0},{1,5},{5... | collective-permute-start | bytes 3145736 | tf_op jit(solution)/shard_map/ppermute | solution.py:14
  299.8 128.3 %copy-start.1 = (bf16[512,1024]{1,0:T(8,128)(2,1)S(1)}, bf16[512,1024]{1,0:T(8,128)(2,1)}, u32[]{:S(2)}) copy-start(bf16[512,1024]{1,0:T(8,128)(2,1)} %fusion.23) | copy-start | bytes 3145732
  299.8 186.7 %all-gather.18.cloned.1.call-start = ((), (), s32[]{:S(2)}) async-start(), calls=%async_computation.5 | async-start | bytes 5242880 | tf_op jit(solution)/shard_map/all_gather | solution.py:84
  315.2 25.6 %collective-permute-start.3 = (bf16[512,1024]{1,0:T(8,128)(2,1)}, bf16[512,1024]{1,0:T(8,128)(2,1)S(1)}, u32[]{:S(2)}, u32[]{:S(2)}) collective-permute-start(bf16[512,1024]{1,0:T(8,128)(2,1)} %collective-permute-done.2), channel_id=1, source_target_pairs={{0,4},{4,8},{8,12},{12,16},{16,20},{20,24},{24,28},{28,0},{1,5},{5... | collective-permute-start | bytes 3145736 | tf_op jit(solution)/shard_map/ppermute | solution.py:14
  341.9 24.6 %collective-permute-start.4 = (bf16[512,1024]{1,0:T(8,128)(2,1)S(1)}, bf16[512,1024]{1,0:T(8,128)(2,1)S(1)}, u32[]{:S(2)}, u32[]{:S(2)}) collective-permute-start(bf16[512,1024]{1,0:T(8,128)(2,1)S(1)} %collective-permute-done.3), channel_id=1, source_target_pairs={{0,4},{4,8},{8,12},{12,16},{16,20},{20,24},{24,28},{28,0},{1,5},{5... | collective-permute-start | bytes 3145736 | tf_op jit(solution)/shard_map/ppermute | solution.py:14
  367.4 23.8 %collective-permute-start.5 = (bf16[512,1024]{1,0:T(8,128)(2,1)S(1)}, bf16[512,1024]{1,0:T(8,128)(2,1)}, u32[]{:S(2)}, u32[]{:S(2)}) collective-permute-start(bf16[512,1024]{1,0:T(8,128)(2,1)S(1)} %collective-permute-done.4), channel_id=1, source_target_pairs={{0,4},{4,8},{8,12},{12,16},{16,20},{20,24},{24,28},{28,0},{1,5},{5... | collective-permute-start | bytes 3145736 | tf_op jit(solution)/shard_map/ppermute | solution.py:14
  391.3 23.2 %collective-permute-start.6 = (bf16[512,1024]{1,0:T(8,128)(2,1)}, bf16[512,1024]{1,0:T(8,128)(2,1)}, u32[]{:S(2)}, u32[]{:S(2)}) collective-permute-start(bf16[512,1024]{1,0:T(8,128)(2,1)} %collective-permute-done.5), channel_id=1, source_target_pairs={{0,4},{4,8},{8,12},{12,16},{16,20},{20,24},{24,28},{28,0},{1,5},{5... | collective-permute-start | bytes 3145736 | tf_op jit(solution)/shard_map/ppermute | solution.py:14
  439.7 172.5 %all-gather.20.cloned.1.call-start = ((), (), s32[]{:S(2)}) async-start(), calls=%async_computation.6 | async-start | bytes 5242880 | tf_op jit(solution)/shard_map/all_gather | solution.py:78
  439.8 23.6 %collective-permute-start.7 = (bf16[512,1024]{1,0:T(8,128)(2,1)}, bf16[512,1024]{1,0:T(8,128)(2,1)S(1)}, u32[]{:S(2)}, u32[]{:S(2)}) collective-permute-start(bf16[512,1024]{1,0:T(8,128)(2,1)} %fusion.26), channel_id=1, source_target_pairs={{0,4},{4,8},{8,12},{12,16},{16,20},{20,24},{24,28},{28,0},{1,5},{5... | collective-permute-start | bytes 3145736 | tf_op jit(solution)/shard_map/ppermute | solution.py:14
  463.4 23.1 %collective-permute-start.8 = (bf16[512,1024]{1,0:T(8,128)(2,1)S(1)}, bf16[512,1024]{1,0:T(8,128)(2,1)}, u32[]{:S(2)}, u32[]{:S(2)}) collective-permute-start(bf16[512,1024]{1,0:T(8,128)(2,1)S(1)} %collective-permute-done.7), channel_id=1, source_target_pairs={{0,4},{4,8},{8,12},{12,16},{16,20},{20,24},{24,28},{28,0},{1,5},{5... | collective-permute-start | bytes 3145736 | tf_op jit(solution)/shard_map/ppermute | solution.py:14
  486.5 23.3 %collective-permute-start.9 = (bf16[512,1024]{1,0:T(8,128)(2,1)}, bf16[512,1024]{1,0:T(8,128)(2,1)}, u32[]{:S(2)}, u32[]{:S(2)}) collective-permute-start(bf16[512,1024]{1,0:T(8,128)(2,1)} %collective-permute-done.8), channel_id=1, source_target_pairs={{0,4},{4,8},{8,12},{12,16},{16,20},{20,24},{24,28},{28,0},{1,5},{5... | collective-permute-start | bytes 3145736 | tf_op jit(solution)/shard_map/ppermute | solution.py:14
  509.8 23.5 %collective-permute-start.10 = (bf16[512,1024]{1,0:T(8,128)(2,1)}, bf16[512,1024]{1,0:T(8,128)(2,1)S(1)}, u32[]{:S(2)}, u32[]{:S(2)}) collective-permute-start(bf16[512,1024]{1,0:T(8,128)(2,1)} %collective-permute-done.9), channel_id=1, source_target_pairs={{0,4},{4,8},{8,12},{12,16},{16,20},{20,24},{24,28},{28,0},{1,5},{5... | collective-permute-start | bytes 3145736 | tf_op jit(solution)/shard_map/ppermute | solution.py:14
  533.3 22.4 %collective-permute-start.11 = (bf16[512,1024]{1,0:T(8,128)(2,1)S(1)}, bf16[512,1024]{1,0:T(8,128)(2,1)S(1)}, u32[]{:S(2)}, u32[]{:S(2)}) collective-permute-start(bf16[512,1024]{1,0:T(8,128)(2,1)S(1)} %collective-permute-done.10), channel_id=1, source_target_pairs={{0,4},{4,8},{8,12},{12,16},{16,20},{20,24},{24,28},{28,0},{1,5},{5... | collective-permute-start | bytes 3145736 | tf_op jit(solution)/shard_map/ppermute | solution.py:14
  556.7 23.1 %collective-permute-start.12 = (bf16[512,1024]{1,0:T(8,128)(2,1)S(1)}, bf16[512,1024]{1,0:T(8,128)(2,1)}, u32[]{:S(2)}, u32[]{:S(2)}) collective-permute-start(bf16[512,1024]{1,0:T(8,128)(2,1)S(1)} %collective-permute-done.11), channel_id=1, source_target_pairs={{0,4},{4,8},{8,12},{12,16},{16,20},{20,24},{24,28},{28,0},{1,5},{5... | collective-permute-start | bytes 3145736 | tf_op jit(solution)/shard_map/ppermute | solution.py:14
  579.8 17.8 %collective-permute-start.13 = (bf16[512,1024]{1,0:T(8,128)(2,1)}, bf16[512,1024]{1,0:T(8,128)(2,1)}, u32[]{:S(2)}, u32[]{:S(2)}) collective-permute-start(bf16[512,1024]{1,0:T(8,128)(2,1)} %collective-permute-done.12), channel_id=1, source_target_pairs={{0,4},{4,8},{8,12},{12,16},{16,20},{20,24},{24,28},{28,0},{1,5},{5... | collective-permute-start | bytes 3145736 | tf_op jit(solution)/shard_map/ppermute | solution.py:14
  620.8 101.6 %collective-permute-start.14 = (f32[512,512]{1,0:T(8,128)S(1)}, f32[512,512]{1,0:T(8,128)}, u32[]{:S(2)}, u32[]{:S(2)}) collective-permute-start(f32[512,512]{1,0:T(8,128)S(1)} %get-tuple-element.9), channel_id=1, source_target_pairs={{0,0},{1,8},{2,16},{3,24},{4,4},{5,12},{6,20},{7,28},{8,1},{9,9},{... | collective-permute-start | bytes 3145736 | tf_op jit(solution)/shard_map/ppermute | solution.py:45
  622.5 101.4 %collective-permute-start.15 = (f32[512,512]{1,0:T(8,128)S(1)}, f32[512,512]{1,0:T(8,128)S(1)}, u32[]{:S(2)}, u32[]{:S(2)}) collective-permute-start(f32[512,512]{1,0:T(8,128)S(1)} %get-tuple-element.8), channel_id=1, source_target_pairs={{0,4},{1,12},{2,20},{3,28},{4,0},{5,8},{6,16},{7,24},{8,5},{9,13},... | collective-permute-start | bytes 3145736 | tf_op jit(solution)/shard_map/ppermute | solution.py:45
  (6 other events, 173.1 us)
Sparse Core Ops, SparseCore 0:
  11.6 37.4 all-gather.7
  51.8 124.4 all-gather.9
  188.6 32.6 all-gather.11
  233.3 34.4 all-gather.13
  299.9 34.9 all-gather.15
  439.8 30.5 all-gather.17
  499.8 34.9 all-gather.19
